TPU v7x, 32 devices: a whole 2x2x4 slice. The times are simulated.
32 devices in a mesh: rows: 8 (over y, x, core), sub: 4 (over z).
Axes of the slice: x: 2, y: 2, z: 4, core: 2. Of those that a mesh axis runs over, the one named last changes fastest.
Arguments:
- u_fem: float32 [120, 524288], P(None, ('rows', 'sub')), may hold values from -600 to 600
- resid_fem: float32 [1, 524288], P(None, ('rows', 'sub')), may hold values from -60 to 60
- slot_map: int32 [32, 32], P(('rows', 'sub')), may hold values from 0 to 31, as said below
- restart: float32 [120, 40], replicated, may hold values from -0.5 to 0.5
- coeff: float32 [3, 120, 120], P(None, None, 'sub'), may hold values from -6 to 6
Outputs:
- new_basis: float32 [40, 524288], P(None, ('rows', 'sub'))
- next_vector: float32 [1, 524288], P(None, ('rows', 'sub'))
- new_coeff: float32 [3, 40, 120], replicated
Inputs may be any that keep to these rules, and one draw needn't show every extreme that they name: Each row of slot_map is a permutation of 0 to 31.
All inputs are finite; a program needn't handle non-finite values.
Results may differ from a plain program's by a relative error of at most 0.00015.
Values sent between devices are 32-bit elements; how exact they have to be, the bound alone decides.
A program may use at most 64 MiB of HBM per device.

v0:
```python
import jax
import jax.numpy as jnp
from jax import lax
from jax.sharding import PartitionSpec as P


def settle(values, source, dev_count):
    width = values.shape[0]
    block_len = values.shape[1] // dev_count
    blocks = values.reshape(width, dev_count, block_len)
    return jnp.take(blocks, source, axis=1).reshape(width, dev_count * block_len)


def local(u_fem, resid_fem, slot_map, restart, coeff):
    highest = lax.Precision.HIGHEST
    dev_count = lax.axis_size(("rows", "sub"))
    nrows_all = u_fem.shape[1] * dev_count
    source = jnp.argsort(slot_map[0])
    basis_rows, resid_row = (u_fem, resid_fem)
    gram_local = jnp.einsum("kn,jn->kj", basis_rows, basis_rows, precision=highest)
    inner_local = jnp.einsum("kn,n->k", basis_rows, resid_row[0], precision=highest)
    gram_sum = lax.psum(gram_local, ("rows", "sub"))
    chol_lower = jnp.linalg.cholesky(gram_sum / nrows_all)
    factor = lax.linalg.triangular_solve(
        chol_lower, restart, left_side=True, lower=True, transpose_a=True
    )
    new_rows = jnp.einsum("kp,kn->pn", factor, basis_rows, precision=highest)
    inner_prod = lax.psum(inner_local, ("rows", "sub"))
    half_solve = lax.linalg.triangular_solve(
        chol_lower, inner_prod[:, None], left_side=True, lower=True
    )
    proj_coef = (
        lax.linalg.triangular_solve(
            chol_lower, half_solve, left_side=True, lower=True, transpose_a=True
        )[:, 0]
        / nrows_all
    )
    remainder = resid_row - jnp.einsum("k,kn->n", proj_coef, basis_rows, precision=highest)[None, :]
    norm_sum = lax.psum(jnp.sum(remainder * remainder), ("rows", "sub"))
    next_row = remainder * lax.rsqrt(norm_sum / nrows_all + 1e-06)
    new_rows, next_row = (
        lax.all_to_all(new_rows, ("rows", "sub"), split_axis=1, concat_axis=1, tiled=True),
        lax.all_to_all(next_row, ("rows", "sub"), split_axis=1, concat_axis=1, tiled=True),
    )
    new_rows = settle(new_rows, source, dev_count)
    next_row = settle(next_row, source, dev_count)
    raised = jnp.dot(chol_lower, restart, precision=highest)
    coeff_all = lax.all_gather(coeff, "sub", axis=2, tiled=True)
    rotated = jnp.einsum("kp,ikm->ipm", raised, coeff_all, precision=highest)
    new_coeff = rotated * lax.rsqrt(jnp.mean(rotated * rotated) + 1e-06)
    return (new_rows, next_row, new_coeff)


def solution(mesh):
    in_specs = (
        P(None, ("rows", "sub")),
        P(None, ("rows", "sub")),
        P(("rows", "sub"), None),
        P(),
        P(None, None, "sub"),
    )
    out_specs = (P(None, ("rows", "sub")), P(None, ("rows", "sub")), P())
    return jax.shard_map(local, mesh=mesh, in_specs=in_specs, out_specs=out_specs, check_vma=False)
```

profile of v0, /device:TPU:0, one launch (start us, length us, event | category | flops | bytes accessed | tf_op | source)
XLA Modules:
  0.0 229.9 jit_solution(9403381852364649270)
XLA Ops:
  0.6 0.0 copy-start
  0.6 0.0 copy-start.1
  0.7 0.0 copy-start.2
  0.7 10.1 %fusion.16 = f32[120,120]{0,1:T(8,128)S(1)} fusion(f32[120,16384]{1,0:T(8,128)} %param.5), kind=kOutput, calls=%fused_computation.44 | convolution fusion | flops 2831155200 | bytes 7921920 | tf_op jit(solution)/shard_map/kn,jn->kj/dot_general | solution.py:20
  10.7 0.0 copy-done.1
  10.7 0.0 copy-done.2
  10.8 6.2 %convolution_bitcast_fusion.3 = f32[120]{0:T(128)S(1)} fusion(f32[120,16384]{1,0:T(8,128)S(1)} %copy-done.1, f32[1,16384]{1,0:T(1,128)S(1)} %copy-done.2), kind=kOutput, calls=%fused_computation.10 | convolution fusion | flops 23592960 | bytes 7930336 | tf_op jit(solution)/shard_map/kn,n->k/dot_general | solution.py:21
  16.9 42.8 %all-reduce = (f32[120,120]{0,1:T(8,128)S(1)}, f32[120]{0:T(128)S(1)}) all-reduce(f32[120,120]{0,1:T(8,128)S(1)} %fusion.16, f32[120]{0:T(128)S(1)} %convolution_bitcast_fusion.3), channel_id=1, replica_groups=mesh['rows'=8,'sub'=4] {'rows','sub'}, use_global_device_ids=true, to_apply=%region_1.2 | all-reduce | flops 14520 | bytes 116160 | tf_op jit(solution)/shard_map/psum | solution.py:22
  59.8 0.1 copy.18
  59.9 11.0 %cholesky.16 = f32[120,120]{1,0:T(8,128)S(1)} custom-call(f32[120,120]{1,0:T(8,128)S(1)} %fusion.9), custom_call_target="Cholesky" | custom-call | tf_op jit(solution)/shard_map/jit(cholesky)/cholesky | solution.py:23
  70.9 0.6 compare_reduce_fusion
  71.5 0.7 select_bitcast_fusion
  72.2 9.2 %custom-call.10 = f32[1,120,120]{1,2,0:T(8,128)S(1)} custom-call(f32[1,120,120]{2,1,0:T(8,128)S(1)} %select_bitcast_fusion), custom_call_target="InvertDiagBlocksLowerTriangular" | custom-call | tf_op jit(solution)/shard_map/triangular_solve | solution.py:24
  81.4 0.2 convolution_bitcast_fusion.2
  81.6 0.2 fusion.1
  81.8 6.7 %multiply_reduce_fusion = (f32[]{:T(128)}, f32[1,16384]{1,0:T(1,128)S(1)}) fusion(f32[1,16384]{1,0:T(1,128)S(1)} %copy-done.2, f32[120,1]{0,1:T(1,128)S(1)} %fusion.1, f32[120,16384]{1,0:T(8,128)} %param.5), kind=kOutput, calls=%fused_computation.15 | convolution fusion | flops 23642112 | bytes 7995876 | tf_op jit(solution)/shard_map/k,kn->n/dot_general | solution.py:38
  88.5 40.3 %psum.23 = f32[]{:T(128)} all-reduce(f32[]{:T(128)} %get-tuple-element.7), channel_id=1, replica_groups=mesh['rows'=8,'sub'=4] {'rows','sub'}, use_global_device_ids=true, to_apply=%region_6.7 | all-reduce | flops 1 | bytes 8 | tf_op jit(solution)/shard_map/psum | solution.py:39
  129.5 0.7 broadcast_multiply_fusion
  130.1 5.4 %all-to-all-start.1 = ((f32[1,32,512]{2,0,1:T(1,128)}), f32[1,32,512]{2,0,1:T(1,128)S(1)}, u32[]{:S(2)}, u32[]{:S(2)}) async-start(f32[1,32,512]{2,0,1:T(1,128)} %bitcast.14), calls=%async_computation.1 | async-start | bytes 131072 | tf_op jit(solution)/shard_map/all_to_all | solution.py:43
  135.5 0.0 copy-done
  135.6 0.2 fusion.7
  135.8 0.0 copy-start.4
  135.8 6.5 %fusion.17 = f32[40,16384]{1,0:T(8,128)S(1)} fusion(f32[120,40]{0,1:T(8,128)S(1)} %fusion.7, f32[120,16384]{1,0:T(8,128)} %param.5), kind=kOutput, calls=%fused_computation.45 | convolution fusion | flops 943718400 | bytes 10504960 | tf_op jit(solution)/shard_map/kp,kn->pn/dot_general | solution.py:27
  142.3 0.0 copy-start.3
  142.3 1.7 copy.36
  144.1 0.0 copy-done.4
  144.1 1.7 sort.17
  145.8 0.0 all-to-all-done.1
  145.8 5.8 %all-to-all-start = ((f32[40,32,512]{2,0,1:T(8,128)}), f32[40,32,512]{2,0,1:T(8,128)S(1)}, u32[]{:S(2)}, u32[]{:S(2)}) async-start(f32[40,32,512]{2,0,1:T(8,128)} %bitcast.69), calls=%async_computation | async-start | bytes 5242880 | tf_op jit(solution)/shard_map/all_to_all | solution.py:42
  151.6 0.1 broadcast_bitcast_fusion
  151.7 0.1 copy.28
  151.8 0.0 copy-done.3
  151.8 67.3 %all_gather.3 = f32[3,120,120]{1,0,2:T(4,128)S(1)} all-gather(f32[3,120,30]{1,0,2:T(4,128)S(1)} %copy.21), channel_id=1, replica_groups=mesh['rows'=8,'sub'=4] {'sub'}, dimensions={2}, use_global_device_ids=true | all-gather | bytes 216000 | tf_op jit(solution)/shard_map/all_gather | solution.py:48
  219.1 0.9 convolution_bitcast_fusion
  220.0 1.0 multiply_reduce_fusion.1
  221.8 0.1 broadcast_bitcast_fusion.1
  221.9 0.6 multiply_bitcast_fusion
  222.5 0.6 gather_fusion.1
  223.1 0.1 copy.29
  223.2 0.7 broadcast_select_fusion.1
  223.9 0.0 all-to-all-done
  223.9 2.2 gather_fusion
  226.2 2.1 copy.26
  228.2 1.7 broadcast_select_fusion
  (10 shorter events, 0.1 us)
Async XLA Ops:
  0.6 134.9 %copy-start = (f32[120,40]{0,1:T(8,128)S(1)}, f32[120,40]{0,1:T(8,128)}, u32[]{:S(2)}) copy-start(f32[120,40]{0,1:T(8,128)} %param.8) | copy-start | bytes 57604
  0.6 10.1 %copy-start.1 = (f32[120,16384]{1,0:T(8,128)S(1)}, f32[120,16384]{1,0:T(8,128)}, u32[]{:S(2)}) copy-start(f32[120,16384]{1,0:T(8,128)} %param.5) | copy-start | bytes 23592964
  0.7 10.1 %copy-start.2 = (f32[1,16384]{1,0:T(1,128)S(1)}, f32[1,16384]{1,0:T(1,128)}, u32[]{:S(2)}) copy-start(f32[1,16384]{1,0:T(1,128)} %param.6) | copy-start | bytes 196612
  130.1 15.6 %all-to-all-start.1 = ((f32[1,32,512]{2,0,1:T(1,128)}), f32[1,32,512]{2,0,1:T(1,128)S(1)}, u32[]{:S(2)}, u32[]{:S(2)}) async-start(f32[1,32,512]{2,0,1:T(1,128)} %bitcast.14), calls=%async_computation.1 | async-start | bytes 131072 | tf_op jit(solution)/shard_map/all_to_all | solution.py:43
  135.8 8.3 %copy-start.4 = (s32[1,32]{1,0:T(1,128)S(1)}, s32[1,32]{1,0:T(1,128)}, u32[]{:S(2)}) copy-start(s32[1,32]{1,0:T(1,128)} %param.7) | copy-start | bytes 388
  142.3 9.4 %copy-start.3 = (f32[3,120,30]{1,2,0:T(8,128)S(1)}, f32[3,120,30]{1,2,0:T(8,128)}, u32[]{:S(2)}) copy-start(f32[3,120,30]{1,2,0:T(8,128)} %param.9) | copy-start | bytes 129604
  145.8 78.2 %all-to-all-start = ((f32[40,32,512]{2,0,1:T(8,128)}), f32[40,32,512]{2,0,1:T(8,128)S(1)}, u32[]{:S(2)}, u32[]{:S(2)}) async-start(f32[40,32,512]{2,0,1:T(8,128)} %bitcast.69), calls=%async_computation | async-start | bytes 5242880 | tf_op jit(solution)/shard_map/all_to_all | solution.py:42
where the time goes:
time: 231 us; the launch traced here: 230 us
  blocking collectives  150 us (65%)
  matrix products  32 us (14%)
  other arithmetic  27 us (12%)
  starting transfers between devices  11.2 us (5%)
  local copies, waits for them, and re-layouts  7.06 us (3%)
    all_gather x1, blocking collectives, local(): coeff_all = lax.all_gather(coeff, 'sub', axis=2, tiled=True)  67.3 us
    psum x1, blocking collectives, local(): gram_sum = lax.psum(gram_local, ('rows', 'sub'))  42.8 us
    psum x1, blocking collectives, local(): norm_sum = lax.psum(jnp.sum(remainder * remainder), ('rows', 'sub'))  40.3 us
    another operation x3, other arithmetic, local(): chol_lower = jnp.linalg.cholesky(gram_sum / nrows_all)  11.6 us
    dot_general x1, matrix products, local(): jnp.einsum('kn,jn->kj', basis_rows, basis_rows, precision=highest)  10.1 us
    another operation x2, other arithmetic, local(): lax.linalg.triangular_solve(chol_lower, restart, left_side=True, lower=Tr...  9.85 us
    dot_general x1, matrix products, local(): jnp.einsum('k,kn->n', proj_coef, basis_rows, precision=highest)[None, :]  6.74 us
    dot_general x1, matrix products, local(): new_rows = jnp.einsum('kp,kn->pn', factor, basis_rows, precision=highest)  6.51 us
  transfers between devices with their start and end apart: 2, of which 0 were waited for; matrix products, arithmetic and copies ran while one was open for 6% of the time, Pallas kernels for 0%

commit v1 on v0

--- a/solution.py
+++ b/solution.py
@@ -2,6 +2,12 @@
 import jax.numpy as jnp
 from jax import lax
 from jax.sharding import PartitionSpec as P
+
+
+def laid_out(blocks, dim):
+    blocks = jnp.moveaxis(blocks, 0, dim)
+    dims = blocks.shape
+    return blocks.reshape(*dims[:dim], dims[dim] * dims[dim + 1], *dims[dim + 2 :])
 
 
 def settle(values, source, dev_count):
@@ -45,8 +51,22 @@
     new_rows = settle(new_rows, source, dev_count)
     next_row = settle(next_row, source, dev_count)
     raised = jnp.dot(chol_lower, restart, precision=highest)
-    coeff_all = lax.all_gather(coeff, "sub", axis=2, tiled=True)
-    rotated = jnp.einsum("kp,ikm->ipm", raised, coeff_all, precision=highest)
+    devices, mine, extent = (lax.axis_size("sub"), lax.axis_index("sub"), coeff.shape[2])
+    upward = [(i, (i + 1) % devices) for i in range(devices)]
+    left = [(i, (i - 1) % devices) for i in range(devices)]
+    middle = devices // 2
+    parts = {}
+    from_left = from_right = coeff
+    for step in range(middle + 1):
+        next_left = lax.ppermute(from_left, "sub", upward) if step < middle else None
+        next_right = lax.ppermute(from_right, "sub", left) if step < devices - middle - 1 else None
+        parts[-step] = jnp.einsum("kp,ikm->ipm", raised, from_left, precision=highest)
+        if 0 < step < devices - middle:
+            parts[step] = jnp.einsum("kp,ikm->ipm", raised, from_right, precision=highest)
+        from_left, from_right = (next_left, next_right)
+    parts = jnp.stack([parts[k] for k in sorted(parts)])
+    parts = parts[(jnp.arange(devices) - mine + middle) % devices]
+    rotated = laid_out(parts, 2)
     new_coeff = rotated * lax.rsqrt(jnp.mean(rotated * rotated) + 1e-06)
     return (new_rows, next_row, new_coeff)
 

time: 231 us -> 223 us (0.965)
  blocking collectives: 150 us -> 80.3 us
  waiting for transfers between devices: 0.01 us -> 52.6 us
  starting transfers between devices: 11.2 us -> 18.1 us
    all_gather x1 -> x0, blocking collectives: 67.3 us -> none  [local(): coeff_all = lax.all_gather(coeff, 'sub', axis=2, tiled=True)]
    ppermute x0 -> x3, waiting for transfers between devices: none -> 46.4 us  [the longest x2 46.4 us: local(): lax.ppermute(from_left, 'sub', upward)]
    ppermute x0 -> x3, starting transfers between devices: none -> 7.02 us  [the longest x2 4.93 us: local(): lax.ppermute(from_left, 'sub', upward)]
    all_to_all x1, waiting for transfers between devices: 0.01 us -> 6.25 us  [local(): lax.all_to_all(new_rows, ('rows', 'sub'), split_axis=1, concat_axis=1, ti...]
    psum x1, blocking collectives: 42.8 us -> 39.8 us  [local(): gram_sum = lax.psum(gram_local, ('rows', 'sub'))]
  transfers between devices with their start and end apart: 2 -> 5, of which waited for: 0 -> 2; matrix products, arithmetic and copies ran while one was open for 6% -> 28% of each run, Pallas kernels for 0% -> 0%
where the time goes in v1:
time: 223 us; the launch traced here: 220 us
  blocking collectives  80.3 us (36%)
  waiting for transfers between devices  52.6 us (24%)
  matrix products  31.6 us (14%)
  other arithmetic  27 us (12%)
  starting transfers between devices  18.1 us (8%)
  local copies, waits for them, and re-layouts  8.45 us (4%)
  between operations  2.31 us (1%)
    ppermute x2, waiting for transfers between devices, local(): lax.ppermute(from_left, 'sub', upward)  46.4 us
    psum x1, blocking collectives, local(): norm_sum = lax.psum(jnp.sum(remainder * remainder), ('rows', 'sub'))  40.4 us
    psum x1, blocking collectives, local(): gram_sum = lax.psum(gram_local, ('rows', 'sub'))  39.8 us
    another operation x3, other arithmetic, local(): chol_lower = jnp.linalg.cholesky(gram_sum / nrows_all)  11.6 us
    dot_general x1, matrix products, local(): jnp.einsum('kn,jn->kj', basis_rows, basis_rows, precision=highest)  9.92 us
    another operation x2, other arithmetic, local(): lax.linalg.triangular_solve(chol_lower, restart, left_side=True, lower=Tr...  9.85 us
    dot_general x1, matrix products, local(): jnp.einsum('k,kn->n', proj_coef, basis_rows, precision=highest)[None, :]  6.74 us
    dot_general x1, matrix products, local(): new_rows = jnp.einsum('kp,kn->pn', factor, basis_rows, precision=highest)  6.51 us
  transfers between devices with their start and end apart: 5, of which 2 were waited for; matrix products, arithmetic and copies ran while one was open for 28% of the time, Pallas kernels for 0%

profile of v1, /device:TPU:0, one launch (start us, length us, event | category | flops | bytes accessed | tf_op | source)
XLA Modules:
  0.0 220.3 jit_solution(1766234675541413213)
XLA Ops:
  0.6 0.0 copy-start
  0.6 0.0 copy-start.1
  0.7 3.1 %collective-permute-start = (f32[3,120,30]{1,2,0:T(8,128)}, f32[3,120,30]{1,2,0:T(8,128)S(1)}, u32[]{:S(2)}, u32[]{:S(2)}) collective-permute-start(f32[3,120,30]{1,2,0:T(8,128)} %param.9), channel_id=1, source_target_pairs={{0,1},{1,2},{2,3},{3,0},{4,5},{5,6},{6,7},{7,4},{8,9},{9,10},{10,1... | collective-permute-start | bytes 129608 | tf_op jit(solution)/shard_map/ppermute | solution.py:61
  3.8 2.1 collective-permute-start.2
  5.9 9.9 %fusion.16 = f32[120,120]{0,1:T(8,128)S(1)} fusion(f32[120,16384]{1,0:T(8,128)} %param.5), kind=kOutput, calls=%fused_computation.55 | convolution fusion | flops 2831155200 | bytes 7921920 | tf_op jit(solution)/shard_map/kn,jn->kj/dot_general | solution.py:26
  15.8 0.0 copy-start.4
  15.8 6.2 %convolution_bitcast_fusion.7 = f32[120]{0:T(128)S(1)} fusion(f32[120,16384]{1,0:T(8,128)S(1)} %copy-done.1, f32[1,16384]{1,0:T(1,128)S(1)} %copy-done.2), kind=kOutput, calls=%fused_computation.15 | convolution fusion | flops 23592960 | bytes 7930336 | tf_op jit(solution)/shard_map/kn,n->k/dot_general | solution.py:27
  22.0 39.8 %all-reduce = (f32[120,120]{0,1:T(8,128)S(1)}, f32[120]{0:T(128)S(1)}) all-reduce(f32[120,120]{0,1:T(8,128)S(1)} %fusion.16, f32[120]{0:T(128)S(1)} %convolution_bitcast_fusion.7), channel_id=1, replica_groups=mesh['rows'=8,'sub'=4] {'rows','sub'}, use_global_device_ids=true, to_apply=%region_1.2 | all-reduce | flops 14520 | bytes 116160 | tf_op jit(solution)/shard_map/psum | solution.py:28
  61.9 0.1 copy.20
  62.0 11.0 %cholesky.16 = f32[120,120]{1,0:T(8,128)S(1)} custom-call(f32[120,120]{1,0:T(8,128)S(1)} %fusion.7), custom_call_target="Cholesky" | custom-call | tf_op jit(solution)/shard_map/jit(cholesky)/cholesky | solution.py:29
  73.0 0.6 compare_reduce_fusion
  73.6 0.7 select_bitcast_fusion
  74.3 9.2 %custom-call.10 = f32[1,120,120]{1,2,0:T(8,128)S(1)} custom-call(f32[1,120,120]{2,1,0:T(8,128)S(1)} %select_bitcast_fusion), custom_call_target="InvertDiagBlocksLowerTriangular" | custom-call | tf_op jit(solution)/shard_map/triangular_solve | solution.py:30
  83.5 0.2 convolution_bitcast_fusion.6
  83.7 0.2 fusion.1
  83.9 6.7 %multiply_reduce_fusion.1 = (f32[]{:T(128)}, f32[1,16384]{1,0:T(1,128)S(1)}) fusion(f32[1,16384]{1,0:T(1,128)S(1)} %copy-done.2, f32[120,1]{0,1:T(1,128)S(1)} %fusion.1, f32[120,16384]{1,0:T(8,128)} %param.5), kind=kOutput, calls=%fused_computation.21 | convolution fusion | flops 23642112 | bytes 7995876 | tf_op jit(solution)/shard_map/k,kn->n/dot_general | solution.py:44
  90.6 40.4 %psum.23 = f32[]{:T(128)} all-reduce(f32[]{:T(128)} %get-tuple-element.7), channel_id=1, replica_groups=mesh['rows'=8,'sub'=4] {'rows','sub'}, use_global_device_ids=true, to_apply=%region_6.7 | all-reduce | flops 1 | bytes 8 | tf_op jit(solution)/shard_map/psum | solution.py:45
  131.7 0.7 broadcast_multiply_fusion
  132.4 5.4 %all-to-all-start.1 = ((f32[1,32,512]{2,0,1:T(1,128)}), f32[1,32,512]{2,0,1:T(1,128)S(1)}, u32[]{:S(2)}, u32[]{:S(2)}) async-start(f32[1,32,512]{2,0,1:T(1,128)} %bitcast.14), calls=%async_computation.1 | async-start | bytes 131072 | tf_op jit(solution)/shard_map/all_to_all | solution.py:49
  137.8 1.6 sort.17
  139.5 0.2 fusion.5
  139.7 0.0 copy-start.3
  139.7 6.5 %fusion.17 = f32[40,16384]{1,0:T(8,128)S(1)} fusion(f32[120,40]{0,1:T(8,128)S(1)} %fusion.5, f32[120,16384]{1,0:T(8,128)} %param.5), kind=kOutput, calls=%fused_computation.56 | convolution fusion | flops 943718400 | bytes 10504960 | tf_op jit(solution)/shard_map/kp,kn->pn/dot_general | solution.py:33
  146.3 0.9 convolution_bitcast_fusion.4
  147.2 1.7 copy.33
  148.9 0.2 convolution_bitcast_fusion.1
  149.1 5.6 %all-to-all-start = ((f32[40,32,512]{2,0,1:T(8,128)}), f32[40,32,512]{2,0,1:T(8,128)S(1)}, u32[]{:S(2)}, u32[]{:S(2)}) async-start(f32[40,32,512]{2,0,1:T(8,128)} %bitcast.94), calls=%async_computation | async-start | bytes 5242880 | tf_op jit(solution)/shard_map/all_to_all | solution.py:48
  154.8 0.1 broadcast_bitcast_fusion
  154.8 0.1 broadcast_bitcast_fusion.1
  154.9 0.1 copy.29
  155.0 0.0 collective-permute-done
  155.0 1.8 collective-permute-start.1
  156.9 0.2 convolution_bitcast_fusion.2
  157.0 0.0 collective-permute-done.2
  157.0 0.2 convolution_bitcast_fusion
  157.2 46.4 %collective-permute-done.1 = f32[3,120,30]{1,2,0:T(8,128)S(1)} collective-permute-done((f32[3,120,30]{1,2,0:T(8,128)S(1)}, f32[3,120,30]{1,2,0:T(8,128)S(1)}, u32[]{:S(2)}, u32[]{:S(2)}) %collective-permute-start.1) | collective-permute-done | bytes 43232 | tf_op jit(solution)/shard_map/ppermute | solution.py:61
  203.6 0.2 convolution_bitcast_fusion.3
  203.8 0.6 gather_fusion.2
  204.4 0.7 multiply_reduce_fusion
  205.8 0.2 copy.23
  205.9 0.8 mul.33
  206.7 0.6 gather_fusion.1
  207.3 0.1 copy.30
  207.4 0.7 broadcast_select_fusion.1
  208.1 6.2 %all-to-all-done = f32[40,32,512]{2,0,1:T(8,128)S(1)} async-done(((f32[40,32,512]{2,0,1:T(8,128)}), f32[40,32,512]{2,0,1:T(8,128)S(1)}, u32[]{:S(2)}, u32[]{:S(2)}) %all-to-all-start) | async-done | bytes 2621472 | tf_op jit(solution)/shard_map/all_to_all | solution.py:48
  214.4 2.2 %gather_fusion = f32[32,40,512]{2,1,0:T(8,128)} fusion(f32[40,32,512]{2,0,1:T(8,128)S(1)} %all-to-all-done, s32[1024]{0:T(1024)S(1)} %pad_clamp_fusion.1), kind=kCustom, calls=%fused_computation | custom fusion | bytes 5243008 | tf_op jit(solution)/shard_map/jit(_take)/gather | solution.py:17
  216.6 2.0 copy.27
  218.6 1.7 broadcast_select_fusion
  (20 shorter events, 0.2 us)
Async XLA Ops:
  0.6 138.8 %copy-start = (f32[120,40]{0,1:T(8,128)S(1)}, f32[120,40]{0,1:T(8,128)}, u32[]{:S(2)}) copy-start(f32[120,40]{0,1:T(8,128)} %param.8) | copy-start | bytes 57604
  0.6 15.2 %copy-start.1 = (f32[120,16384]{1,0:T(8,128)S(1)}, f32[120,16384]{1,0:T(8,128)}, u32[]{:S(2)}) copy-start(f32[120,16384]{1,0:T(8,128)} %param.5) | copy-start | bytes 23592964
  0.7 15.1 %copy-start.2 = (f32[1,16384]{1,0:T(1,128)S(1)}, f32[1,16384]{1,0:T(1,128)}, u32[]{:S(2)}) copy-start(f32[1,16384]{1,0:T(1,128)} %param.6) | copy-start | bytes 196612
  0.7 154.4 %collective-permute-start = (f32[3,120,30]{1,2,0:T(8,128)}, f32[3,120,30]{1,2,0:T(8,128)S(1)}, u32[]{:S(2)}, u32[]{:S(2)}) collective-permute-start(f32[3,120,30]{1,2,0:T(8,128)} %param.9), channel_id=1, source_target_pairs={{0,1},{1,2},{2,3},{3,0},{4,5},{5,6},{6,7},{7,4},{8,9},{9,10},{10,1... | collective-permute-start | bytes 129608 | tf_op jit(solution)/shard_map/ppermute | solution.py:61
  3.8 153.3 %collective-permute-start.2 = (f32[3,120,30]{1,2,0:T(8,128)}, f32[3,120,30]{1,2,0:T(8,128)S(1)}, u32[]{:S(2)}, u32[]{:S(2)}) collective-permute-start(f32[3,120,30]{1,2,0:T(8,128)} %param.9), channel_id=1, source_target_pairs={{0,3},{1,0},{2,1},{3,2},{4,7},{5,4},{6,5},{7,6},{8,11},{9,8},{10,9... | collective-permute-start | bytes 129608 | tf_op jit(solution)/shard_map/ppermute | solution.py:62
  15.8 122.0 %copy-start.4 = (s32[1,32]{1,0:T(1,128)S(1)}, s32[1,32]{1,0:T(1,128)}, u32[]{:S(2)}) copy-start(s32[1,32]{1,0:T(1,128)} %param.7) | copy-start | bytes 388
  132.4 16.7 %all-to-all-start.1 = ((f32[1,32,512]{2,0,1:T(1,128)}), f32[1,32,512]{2,0,1:T(1,128)S(1)}, u32[]{:S(2)}, u32[]{:S(2)}) async-start(f32[1,32,512]{2,0,1:T(1,128)} %bitcast.14), calls=%async_computation.1 | async-start | bytes 131072 | tf_op jit(solution)/shard_map/all_to_all | solution.py:49
  139.7 9.2 %copy-start.3 = (f32[3,120,30]{1,2,0:T(8,128)S(1)}, f32[3,120,30]{1,2,0:T(8,128)}, u32[]{:S(2)}) copy-start(f32[3,120,30]{1,2,0:T(8,128)} %param.9) | copy-start | bytes 129604
  149.1 65.3 %all-to-all-start = ((f32[40,32,512]{2,0,1:T(8,128)}), f32[40,32,512]{2,0,1:T(8,128)S(1)}, u32[]{:S(2)}, u32[]{:S(2)}) async-start(f32[40,32,512]{2,0,1:T(8,128)} %bitcast.94), calls=%async_computation | async-start | bytes 5242880 | tf_op jit(solution)/shard_map/all_to_all | solution.py:48
  155.0 48.6 %collective-permute-start.1 = (f32[3,120,30]{1,2,0:T(8,128)S(1)}, f32[3,120,30]{1,2,0:T(8,128)S(1)}, u32[]{:S(2)}, u32[]{:S(2)}) collective-permute-start(f32[3,120,30]{1,2,0:T(8,128)S(1)} %collective-permute-done), channel_id=1, source_target_pairs={{0,1},{1,2},{2,3},{3,0},{4,5},{5,6},{6,7},{7,4},{8,9},{9,10},{10,1... | collective-permute-start | bytes 129608 | tf_op jit(solution)/shard_map/ppermute | solution.py:61
